TPU v7x, 32 devices: a whole 2x2x4 slice. The times are simulated.
32 devices in a mesh: band: 2 (over core), tmpl: 8 (over z, x), tm: 2 (over y).
Axes of the slice: x: 2, y: 2, z: 4, core: 2. Of those that a mesh axis runs over, the one named last changes fastest.
Arguments:
- strain_high: float32 [16384], P('tm'), may hold values from -6 to 6
- strain_mid: float32 [2048], P('tm'), may hold values from -6 to 6
- strain_low: float32 [256], P('tm'), may hold values from -6 to 6
- filters_high: float32 [320, 1024], P('tmpl'), may hold values from -0.1875 to 0.1875
- filters_mid: float32 [320, 1024], P('tmpl'), may hold values from -0.1875 to 0.1875
- filters_low: float32 [320, 128], P('tmpl'), may hold values from -0.5 to 0.5
- recon_high: float32 [320, 2, 2048], P(None, None, 'tmpl'), may hold values from -0.3125 to 0.3125
- recon_mid: float32 [320, 2, 2048], P(None, None, 'tmpl'), may hold values from -0.3125 to 0.3125
- recon_low: float32 [320, 2, 2048], P(None, None, 'tmpl'), may hold values from -0.3125 to 0.3125
- basis_count: int32 [3], replicated, may hold values from 160 to 320
Outputs:
- snr: float32 [2, 2048, 16384], P('band', 'tmpl', 'tm')
Inputs may be any that keep to these rules, and one draw needn't show every extreme that they name: basis_count[b] says how many of the first 320 basis vectors band b uses.
All inputs are finite; a program needn't handle non-finite values.
Results may differ from a plain program's by a relative error of at most 0.000082.
Values sent between devices are 32-bit elements; how exact they have to be, the bound alone decides.
A program may use at most 128 MiB of HBM per device.

v0:
```python
import functools
import math

import jax
import jax.numpy as jnp
import numpy as np
from jax import lax
from jax.experimental import pallas as pl
from jax.experimental.pallas import tpu as pltpu
from jax.sharding import PartitionSpec as P

RATIO = 8
HALF_TAPS = 8
LANES = 128
WIDE = 256
MESH = pl.DeviceIdType.MESH


def upsample_matrix(rows, cols):
    u = np.arange(rows)[:, None]
    v = np.arange(cols)[None, :]
    lag = u - v // RATIO
    offset = (v % RATIO) / RATIO - (lag - HALF_TAPS)
    value = np.sinc(offset) * (0.5 + 0.5 * np.cos(np.pi * offset / (HALF_TAPS + 1)))
    return np.where((lag >= 0) & (lag < 2 * HALF_TAPS), value, 0.0).astype(np.float32)


def gather_kernel(
    sizes, count_ref, low_ref, mid_ref, high_ref, sl_ref, sm_ref, sh_ref, g_top, g_rest,
    recon_low, recon_mid, recon_high,
    w_top, w_rest, p_top, p_rest, frames_top, frames_rest,
    low_all, mid_all, high_all, sl_all, sm_all, sh_prev,
    low_r, mid_r, high_r, recon_sem, frame_sem, x_full,
    fl_top, fl_rest, fm_top, fm_rest, fh_top, fh_rest,
    strain_send, strain_recv, lz_send, lz_recv, lx_send, lx_recv,
    z_send, z_recv, x_send, x_recv, y_send, y_recv, d_send, d_recv, c_send, c_recv,
):
    bands, peers, slices, lines, parts = sizes
    rings = peers // lines
    b, p, y = lax.axis_index("band"), lax.axis_index("tmpl"), lax.axis_index("tm")
    z, x = p // lines, p % lines
    part = y % parts

    def along_z(k):
        return (b, ((z + k) % rings) * lines + x, y)

    def along_y(m):
        return (b, p, y - part + (part + m) % parts)

    across = (b, z * lines + (x + 1) % lines, y)
    sibling = (1 - b, p, y)
    barrier = pltpu.get_barrier_semaphore()
    others = [along_z(k) for k in range(1, rings)] + [sibling]
    others += [(b, p, (y + k) % slices) for k in range(1, slices)]
    if lines > 1:
        others += [across]
    for device in others:
        pl.semaphore_signal(barrier, inc=1, device_id=device, device_id_type=MESH)
    pl.semaphore_wait(barrier, len(others))

    sent, strains, landed = [], [], ([], [])

    def send(src, dst, sems, at, device):
        copy = pltpu.make_async_remote_copy(
            src_ref=src, dst_ref=dst, send_sem=sems[0].at[at], recv_sem=sems[1].at[at],
            device_id=device, device_id_type=MESH,
        )
        copy.start()
        sent.append(copy)
        return copy

    strain = (strain_send, strain_recv)
    for k in range(1, slices):
        device = (b, p, (y + k) % slices)
        strains.append(send(sl_ref, sl_all.at[2 + y], strain, (0, k), device))
        strains.append(send(sm_ref, sm_all.at[2 + y], strain, (1, k), device))
    if slices > 1:
        tail = sh_prev.shape[0]
        last = sh_ref.at[pl.ds(sh_ref.shape[0] - tail, tail)]
        strains.append(send(last, sh_prev, strain, (2, 1), (b, p, (y + 1) % slices)))

    arrays = ((mid_ref, mid_all), (high_ref, high_all))
    size = [ref.shape[1] // (bands * parts) for ref, _ in arrays]

    def cols(a, m=0):
        start = (b * parts + (part + m) % parts) * size[a]
        return pl.ds(pl.multiple_of(start, LANES), size[a])

    def shard(k, other=0):
        return ((z + rings - k) % rings) * lines + (x + other) % lines

    low_z = {k: send(low_ref, low_all.at[p], (lz_send, lz_recv), k, along_z(k)) for k in range(1, rings)}
    from_z, from_x, from_y, from_d = {}, {}, {}, {}
    low_x = {}
    if lines > 1:
        low_x[0] = send(low_ref, low_all.at[p], (lx_send, lx_recv), 0, across)
    for a, (ref, full) in enumerate(arrays):
        for k in range(1, rings):
            from_z[a, k] = send(
                ref.at[:, cols(a)], full.at[p, :, cols(a)], (z_send, z_recv), (a, k), along_z(k)
            )
        if lines > 1:
            for m in range(parts):
                piece = send(
                    ref.at[:, cols(a, m)], full.at[p, :, cols(a, m)],
                    (x_send, x_recv) if m == 0 else (d_send, d_recv), (a, m, 0), across,
                )
                (from_x if m == 0 else from_d)[a, m, 0] = piece
    low_all[p] = low_ref[...]
    mid_all[p] = mid_ref[...]
    high_all[p] = high_ref[...]
    for ref, value in ((sl_all, sl_ref), (sm_all, sm_ref)):
        zero = jnp.zeros(value.shape, jnp.float32)
        ref[0] = zero
        ref[1] = zero
        ref[slices + 2] = zero
        ref[slices + 3] = zero
        ref[2 + y] = value[...]
    if slices == 1:
        sh_prev[...] = jnp.zeros(sh_prev.shape, jnp.float32)

    count = [0]

    def pass_on(a, view):
        at = (a, count[0])
        count[0] += 1
        landed[a].append(send(view, view, (c_send, c_recv), at, sibling))

    recons = []
    for i, (src, dst) in enumerate(((recon_low, low_r), (recon_mid, mid_r), (recon_high, high_r))):
        copy = pltpu.make_async_copy(src.at[:, b, :], dst, recon_sem.at[i])
        copy.start()
        recons.append(copy)
    for copy in strains:
        copy.wait_recv()
    before = sh_prev.shape[0]
    x_full[:before] = jnp.where(y > 0, sh_prev[...], 0.0)
    x_full[before:] = sh_ref[...]
    chunks = fh_top.shape[0] // LANES - 1
    stride = -(-chunks // 3)
    stores = []

    def frames_part(i):
        first, last = i * stride, min(chunks, (i + 1) * stride)
        fill_frames(lambda r: x_full[pl.ds(r, 1), :], fh_top, fh_rest, chunks, first, last)
        low, high = (chunks + 1 - last) * LANES if last < chunks else 0, (chunks + 1 - first) * LANES
        for j, (src, dst) in enumerate(((fh_top, frames_top), (fh_rest, frames_rest))):
            rows = pl.ds(low, high - low)
            copy = pltpu.make_async_copy(src.at[rows], dst.at[rows], frame_sem.at[i, j])
            copy.start()
            stores.append(copy)

    frames_part(0)
    for k in range(1, rings):
        low_z[k].wait_recv()
        if lines > 1:
            view = low_all.at[shard(k)]
            low_x[k] = send(view, view, (lx_send, lx_recv), k, across)
    for a, (_, full) in enumerate(arrays):
        count[0] = 0
        for k in range(1, rings):
            from_z[a, k].wait_recv()
            view = full.at[shard(k), :, cols(a)]
            if lines > 1:
                from_x[a, 0, k] = send(view, view, (x_send, x_recv), (a, 0, k), across)
            for m in range(1, parts):
                from_y[a, m, k] = send(view, view, (y_send, y_recv), (a, m, k), along_y(m))
            pass_on(a, view)
    base = count[0]
    frames_part(1)
    for a, (_, full) in enumerate(arrays):
        count[0] = base
        for k in range(rings):
            if lines > 1:
                from_x[a, 0, k].wait_recv()
                view = full.at[shard(k, 1), :, cols(a)]
                if k > 0:
                    for m in range(1, parts):
                        from_d[a, m, k] = send(view, view, (d_send, d_recv), (a, m, k), along_y(m))
                pass_on(a, view)
            for m in range(1, parts):
                if k == 0:
                    continue
                from_y[a, m, k].wait_recv()
                view = full.at[shard(k), :, cols(a, parts - m)]
                pass_on(a, view)
    base = count[0]
    frames_part(2)

    def last_pieces(a, full):
        count[0] = base
        for k in range(rings):
            for m in range(1, parts):
                if lines > 1:
                    from_d[a, m, k].wait_recv()
                    shift = m if k == 0 else parts - m
                    pass_on(a, full.at[shard(k, 1), :, cols(a, shift)])

    low_here, mid_here, low_total, mid_total = bounds(sl_ref, sm_ref, slices)
    taps_low, taps_mid = low_ref.shape[1], mid_ref.shape[1]
    low_chunks, mid_chunks = (r.shape[0] // LANES - 1 for r in (fl_top, fm_top))
    rows_mid = mid_here // LANES

    def low_row(r):
        return sl_all[y + 1 - taps_low // LANES + r]

    def mid_row(r):
        at = r + (y + 2) * rows_mid - taps_mid // LANES - 1
        return sm_all[at // rows_mid, pl.ds(at % rows_mid, 1), :]

    fill_frames(shifted(low_row, HALF_TAPS + 1), fl_top, fl_rest, low_chunks)
    fill_frames(shifted(mid_row, HALF_TAPS), fm_top, fm_rest, mid_chunks)
    for copy in recons:
        copy.wait()
    last_pieces(*(0, mid_all))
    for copy in low_x.values():
        copy.wait_recv()
    low_w = split(template_filters(low_r, low_all, count_ref[2]))
    parts_low = []
    for c in range(low_chunks):
        at = (low_chunks - 1 - c) * LANES
        parts_low.append(dot3(low_w, (fl_top[at : at + LANES, :LANES], fl_rest[at : at + LANES, :LANES])))
    low = jnp.concatenate(parts_low, axis=1)
    time = y * low_here - (HALF_TAPS + 1) + lax.broadcasted_iota(jnp.int32, low.shape, 1)
    low = split(jnp.where((time >= 0) & (time < low_total), low, 0.0))
    for copy in landed[0]:
        copy.wait_recv()
    mid_w = split(template_filters(mid_r, mid_all, count_ref[1]))
    last_pieces(*(1, high_all))
    width, columns = g_top.shape[1], p_top.shape[1]
    for start in range(0, columns, WIDE):
        size_here = min(WIDE, columns - start)
        at = (mid_chunks - taps_mid // LANES - start // LANES) * LANES
        frames = (fm_top[at : at + taps_mid, :size_here], fm_rest[at : at + taps_mid, :size_here])
        value = dot3(mid_w, frames)
        base_col, lead = start // width * LANES, start % width
        tile = slice(lead, lead + size_here)
        pieces = tuple(v[:, base_col : base_col + WIDE] for v in low)
        value += dot3(pieces, (g_top[:, tile], g_rest[:, tile]))
        time = y * mid_here - HALF_TAPS + start + lax.broadcasted_iota(jnp.int32, value.shape, 1)
        top, rest = split(jnp.where((time >= 0) & (time < mid_total), value, 0.0))
        p_top[:, start : start + size_here] = top
        p_rest[:, start : start + size_here] = rest
    for copy in landed[1]:
        copy.wait_recv()
    w_top[...], w_rest[...] = split(template_filters(high_r, high_all, count_ref[0]))
    for copy in sent:
        copy.wait_send()
    for copy in stores:
        copy.wait()


def bounds(s_low, s_mid, slices):
    low, mid = s_low.shape[0] * LANES, s_mid.shape[0] * LANES
    return low, mid, low * slices, mid * slices


def template_filters(recon_ref, full, count):
    peers, rows, taps = full.shape
    first = (((0,), (0,)), ((), ()))
    index = lax.broadcasted_iota(jnp.int32, recon_ref.shape, 0)
    recon = jnp.where(index < count, recon_ref[...], 0.0)
    if rows % 8 == 0:
        return dot3(split(recon), split(full[...].reshape(peers * rows, taps)), first)
    total = 0.0
    for p in range(peers):
        total += dot3(split(recon[p * rows : (p + 1) * rows]), split(full[p]), first)
    return total


def gather(sizes, count, filters, strains, g, recons):
    low, mid, high = filters
    s_low, s_mid, s_high = strains
    bands, peers, slices = sizes
    lines = 2 if peers % 2 == 0 else 1
    rings = peers // lines
    parts = math.gcd(slices, min(mid.shape[1], high.shape[1]) // (bands * LANES))
    f32, half = jnp.float32, jnp.bfloat16
    basis, _, tmpl = recons[0].shape
    taps_low, taps_mid, taps = (f.shape[1] for f in filters)
    low_here, mid_here, _, _ = bounds(s_low, s_mid, slices)
    samples = s_high.shape[0] * LANES
    columns = mid_here + LANES
    vmem = pl.BlockSpec(memory_space=pltpu.VMEM)
    anywhere = pl.BlockSpec(memory_space=pl.ANY)
    dma = pltpu.SemaphoreType.DMA

    def two(*dims):
        return [dma(dims)] * 2

    def frames(rows):
        return [pltpu.VMEM((rows, WIDE), half)] * 2

    return pl.pallas_call(
        functools.partial(gather_kernel, (bands, peers, slices, lines, parts)),
        out_shape=[jax.ShapeDtypeStruct((tmpl, taps), half)] * 2
        + [jax.ShapeDtypeStruct((tmpl, columns), half)] * 2
        + [jax.ShapeDtypeStruct((samples + taps, WIDE), half)] * 2,
        in_specs=[pl.BlockSpec(memory_space=pltpu.SMEM)] + [vmem] * 8 + [anywhere] * 3,
        out_specs=[vmem] * 4 + [anywhere] * 2,
        scratch_shapes=[pltpu.VMEM((peers,) + a.shape, f32) for a in filters]
        + [pltpu.VMEM((slices + 4,) + a.shape, f32) for a in (s_low, s_mid)]
        + [pltpu.VMEM((taps // LANES, LANES), f32)]
        + [pltpu.VMEM((basis, tmpl), f32)] * 3
        + [dma((3,)), dma((3, 2)), pltpu.VMEM(((samples + taps) // LANES, LANES), f32)]
        + frames(low_here + 2 * LANES + taps_low) + frames(columns + taps_mid) + frames(samples + taps)
        + two(3, slices) + two(rings) + two(rings) + two(2, rings)
        + two(2, parts, rings) * 3 + two(2, peers * parts),
        compiler_params=pltpu.CompilerParams(
            collective_id=0, has_side_effects=True, vmem_limit_bytes=60 * 1024 * 1024
        ),
        name="gather_filters",
    )(count, *filters, *strains, *g, *recons)


def split(value):
    top = value.astype(jnp.bfloat16)
    return top, (value - top.astype(jnp.float32)).astype(jnp.bfloat16)


def dot3(a, b, dims=(((1,), (0,)), ((), ()))):
    def one(u, v):
        return lax.dot_general(u, v, dims, preferred_element_type=jnp.float32)

    return one(a[0], b[0]) + one(a[0], b[1]) + one(a[1], b[0])


def staggered(row):
    return pltpu.roll(jnp.broadcast_to(row, (LANES, LANES)), 0, 1, stride=1, stride_axis=0)


def shifted(read, by):
    lane = lax.broadcasted_iota(jnp.int32, (1, LANES), 1)

    def row(r):
        late = [pltpu.roll(read(r + i), by, 1) for i in range(2)]
        return jnp.where(lane >= by, late[1], late[0])

    return row


def fill_frames(row, top_ref, rest_ref, chunks, first=0, last=None):
    lane = lax.broadcasted_iota(jnp.int32, (LANES, LANES), 1)
    lag = lax.broadcasted_iota(jnp.int32, (LANES, LANES), 0)

    def step(c, before):
        now = staggered(row(c + 1))
        top, rest = split(jnp.where(lane >= lag, now, before))
        left = pl.multiple_of((chunks - 1 - c) * LANES, LANES)
        right = pl.multiple_of((chunks - c) * LANES, LANES)
        for ref, value in ((top_ref, top), (rest_ref, rest)):
            ref[pl.ds(left, LANES), :LANES] = value
            ref[pl.ds(right, LANES), LANES:] = value
        return now

    lax.fori_loop(first, chunks if last is None else last, step, staggered(row(first)))


def compute_kernel(
    w_top, w_rest, p_top, p_rest, g_top, g_rest, frames_top, frames_rest,
    out_ref, fh_top, fh_rest, frame_sem,
):
    step = pl.program_id(0)
    blocks = pl.num_programs(0)
    taps = w_top.shape[1]
    width = out_ref.shape[2]
    chunks = fh_top.shape[0] // LANES - 1

    def block(j):
        rows = pl.ds(pl.multiple_of(j * width, width), width)
        return [
            pltpu.make_async_copy(src.at[rows], dst.at[rows], frame_sem.at[j, i])
            for i, (src, dst) in enumerate(((frames_top, fh_top), (frames_rest, fh_rest)))
        ]

    total = fh_top.shape[0] // width
    ahead = taps // width

    @pl.when(step == 0)
    def _():
        for j in reversed(range(total)):
            for copy in block(j):
                copy.start()
        for j in range(total - ahead, total):
            for copy in block(j):
                copy.wait()

    for copy in block(blocks - 1 - step):
        copy.wait()
    base = pl.multiple_of(step * (width // RATIO), LANES)
    pieces = (p_top[:, pl.ds(base, WIDE)], p_rest[:, pl.ds(base, WIDE)])
    for start in range(0, width, WIDE):
        at = (chunks - taps // LANES - start // LANES - step * (width // LANES)) * LANES
        rows = pl.ds(pl.multiple_of(at, LANES), taps)
        value = dot3((w_top[...], w_rest[...]), (fh_top[rows, :], fh_rest[rows, :]))
        tile = slice(start, start + WIDE)
        out_ref[0, :, tile] = value + dot3(pieces, (g_top[:, tile], g_rest[:, tile]))


def compute(w, p, g, frames):
    tmpl, taps = w[0].shape
    rows = frames[0].shape[0]
    samples = rows - taps
    width = g[0].shape[1]
    vmem = pl.BlockSpec(memory_space=pltpu.VMEM)
    return pl.pallas_call(
        compute_kernel,
        grid=(samples // width,),
        out_shape=jax.ShapeDtypeStruct((1, tmpl, samples), jnp.float32),
        in_specs=[vmem] * 6 + [pl.BlockSpec(memory_space=pl.ANY)] * 2,
        out_specs=pl.BlockSpec((1, tmpl, width), lambda i: (0, 0, i)),
        scratch_shapes=[pltpu.VMEM((rows, WIDE), jnp.bfloat16)] * 2
        + [pltpu.SemaphoreType.DMA((rows // width, 2))],
        compiler_params=pltpu.CompilerParams(vmem_limit_bytes=60 * 1024 * 1024),
        name="filter_templates",
    )(*w, *p, *g, *frames)


def local(
    sizes, strain_high, strain_mid, strain_low, filters_high, filters_mid, filters_low,
    recon_high, recon_mid, recon_low, basis_count,
):
    matrix = upsample_matrix(WIDE, RATIO * LANES)
    top = matrix.astype(jnp.bfloat16)
    rest = (matrix - top.astype(np.float32)).astype(jnp.bfloat16)
    g = (jnp.asarray(top), jnp.asarray(rest))
    strains = [s.reshape(-1, LANES) for s in (strain_low, strain_mid, strain_high)]
    out = gather(
        sizes, basis_count, (filters_low, filters_mid, filters_high), strains, g,
        (recon_low, recon_mid, recon_high),
    )
    return compute(out[:2], out[2:4], g, out[4:])


def solution(mesh):
    sizes = tuple(mesh.shape[name] for name in ("band", "tmpl", "tm"))
    in_specs = (
        P("tm"), P("tm"), P("tm"),
        P("tmpl", None), P("tmpl", None), P("tmpl", None),
        P(None, None, "tmpl"), P(None, None, "tmpl"), P(None, None, "tmpl"),
        P(),
    )
    return jax.shard_map(
        functools.partial(local, sizes), mesh=mesh, in_specs=in_specs,
        out_specs=P("band", "tmpl", "tm"), check_vma=False,
    )
```

profile of v0, /device:TPU:0, one launch (start us, length us, event | category | flops | bytes accessed | tf_op | source)
XLA Modules:
  0.0 58.1 jit_solution(16769461485872848974)
XLA Ops:
  0.0 35.6 %gather_filters.1 = (bf16[256,1024]{1,0:T(8,128)(2,1)}, bf16[256,1024]{1,0:T(8,128)(2,1)}, bf16[256,1152]{1,0:T(8,128)(2,1)}, bf16[256,1152]{1,0:T(8,128)(2,1)},...) custom-call(s32[3]{0:T(128)} %count_ref.1, f32[40,128]{1,0:T(8,128)} %low_ref.1, f32[40,1024]{1,0:T(8,128)} %mid_ref.1, ...), custom_call_target="tpu_custom_call" | custom-call | tf_op jit(solution)/shard_map/gather_filters/pallas_call | solution.py:294
  35.6 22.5 %filter_templates.1 = f32[1,256,8192]{2,1,0:T(8,128)} custom-call(bf16[256,1024]{1,0:T(8,128)(2,1)} %get-tuple-element.11.w_top, bf16[256,1024]{1,0:T(8,128)(2,1)} %get-tuple-element.12.w_rest, bf16[256,1152]{1,0:T(8,128)(2,1)} %get-tuple-element.13.p_top, bf16[256,1152]{1,0:T(8,128)(2,1)} %get-tuple-element.14.p_rest, ...), custom_call_target="tpu_custom_call" | custom-call | tf_op jit(solution)/shard_map/filter_templates/pallas_call | solution.py:406
where the time goes:
time: 58.5 us; the launch traced here: 58.1 us
  Pallas kernels  58.1 us (99%)
    pallas_call x1, Pallas kernels, gather(): pl.pallas_call(functools.partial(gather_kernel, (bands, peers, slices, li...  35.6 us
    pallas_call x1, Pallas kernels, compute(): pl.pallas_call(compute_kernel, grid=(samples // width,), out_shape=jax.Sh...  22.5 us

commit v1 on v0

v1 whole, which is shorter than its diff:
```python
import functools
import math

import jax
import jax.numpy as jnp
import numpy as np
from jax import lax
from jax.experimental import pallas as pl
from jax.experimental.pallas import tpu as pltpu
from jax.sharding import PartitionSpec as P

RATIO = 8
HALF_TAPS = 8
LANES = 128
WIDE = 256
WINDOW = 2 * WIDE
SPAN = WINDOW // RATIO + 2 * HALF_TAPS
MESH = pl.DeviceIdType.MESH


def upsample_matrix():
    u = np.arange(SPAN)[:, None]
    v = np.arange(WINDOW)[None, :]
    lag = u - v // RATIO
    offset = (v % RATIO) / RATIO - (lag - HALF_TAPS)
    value = np.sinc(offset) * (0.5 + 0.5 * np.cos(np.pi * offset / (HALF_TAPS + 1)))
    value = np.where((lag >= 0) & (lag < 2 * HALF_TAPS), value, 0.0).astype(np.float32)
    top = value.astype(jnp.bfloat16)
    rest = (value - top.astype(np.float32)).astype(jnp.bfloat16)
    pad = np.zeros((WIDE - 3 * SPAN, WINDOW), jnp.bfloat16)
    return np.concatenate([top, top, rest, pad], axis=0)


def products(blocks):
    if blocks == 1:
        return [({0: 1}, (0,), (0,))]
    n = blocks // 2
    inner = products(n)

    def less(frames, shift):
        total = dict(frames)
        total = {m: -c for m, c in frames.items()}
        for m, c in frames.items():
            total[m + shift] = total.get(m + shift, 0) + c
        return {m: c for m, c in total.items() if c}

    both = [(f, w + tuple(i + n for i in w), o + tuple(k + n for k in o)) for f, w, o in inner]
    first = [(less(f, -n), tuple(i + n for i in w), o) for f, w, o in inner]
    last = [(less(f, n), w, tuple(k + n for k in o)) for f, w, o in inner]
    return both + first + last


def gather_kernel(
    sizes, count_ref, low_ref, mid_ref, high_ref, sl_ref, sm_ref, sh_ref, g_ref,
    recon_low, recon_mid, recon_high,
    w_out, p_out, g_out, frames_out,
    low_all, mid_all, high_all, sl_all, sm_all, sh_prev,
    low_r, mid_r, high_r, load_sem, x_full,
    fl_top, fl_rest, fm_top, fm_rest, p_full,
    strain_send, strain_recv, lz_send, lz_recv, lx_send, lx_recv,
    z_send, z_recv, x_send, x_recv, y_send, y_recv, d_send, d_recv, c_send, c_recv,
):
    bands, peers, slices, lines, parts = sizes
    rings = peers // lines
    b, p, y = lax.axis_index("band"), lax.axis_index("tmpl"), lax.axis_index("tm")
    z, x = p // lines, p % lines
    part = y % parts

    def along_z(k):
        return (b, ((z + k) % rings) * lines + x, y)

    def along_y(m):
        return (b, p, y - part + (part + m) % parts)

    across = (b, z * lines + (x + 1) % lines, y)
    sibling = (1 - b, p, y)
    before = sh_prev.shape[0]
    loads = []
    for i, (src, dst) in enumerate((
        (low_ref, low_all.at[p]), (mid_ref, mid_all.at[p]), (high_ref, high_all.at[p]),
        (sl_ref, sl_all.at[2 + y]), (sm_ref, sm_all.at[2 + y]),
        (sh_ref, x_full.at[pl.ds(before, sh_ref.shape[0])]),
        (recon_low.at[:, b, :], low_r), (recon_mid.at[:, b, :], mid_r), (recon_high.at[:, b, :], high_r),
        (g_ref, g_out),
    )):
        copy = pltpu.make_async_copy(src, dst, load_sem.at[i])
        copy.start()
        loads.append(copy)
    barrier = pltpu.get_barrier_semaphore()
    others = [along_z(k) for k in range(1, rings)] + [sibling]
    others += [(b, p, (y + k) % slices) for k in range(1, slices)]
    if lines > 1:
        others += [across]
    for device in others:
        pl.semaphore_signal(barrier, inc=1, device_id=device, device_id_type=MESH)
    pl.semaphore_wait(barrier, len(others))
    for copy in loads[:6]:
        copy.wait()

    sent, strains, landed = [], [], ([], [])

    def send(src, dst, sems, at, device):
        copy = pltpu.make_async_remote_copy(
            src_ref=src, dst_ref=dst, send_sem=sems[0].at[at], recv_sem=sems[1].at[at],
            device_id=device, device_id_type=MESH,
        )
        copy.start()
        sent.append(copy)
        return copy

    strain = (strain_send, strain_recv)
    for k in range(1, slices):
        device = (b, p, (y + k) % slices)
        strains.append(send(sl_all.at[2 + y], sl_all.at[2 + y], strain, (0, k), device))
        strains.append(send(sm_all.at[2 + y], sm_all.at[2 + y], strain, (1, k), device))
    if slices > 1:
        tail = sh_prev.shape[0]
        last = x_full.at[pl.ds(sh_ref.shape[0], tail)]
        strains.append(send(last, sh_prev, strain, (2, 1), (b, p, (y + 1) % slices)))

    arrays = ((mid_ref, mid_all), (high_ref, high_all))
    size = [ref.shape[1] // (bands * parts) for ref, _ in arrays]

    def cols(a, m=0):
        start = (b * parts + (part + m) % parts) * size[a]
        return pl.ds(pl.multiple_of(start, LANES), size[a])

    def shard(k, other=0):
        return ((z + rings - k) % rings) * lines + (x + other) % lines

    low_z = {k: send(low_all.at[p], low_all.at[p], (lz_send, lz_recv), k, along_z(k)) for k in range(1, rings)}
    from_z, from_x, from_y, from_d = {}, {}, {}, {}
    low_x = {}
    if lines > 1:
        low_x[0] = send(low_all.at[p], low_all.at[p], (lx_send, lx_recv), 0, across)
    for a, (ref, full) in enumerate(arrays):
        for k in range(1, rings):
            from_z[a, k] = send(
                full.at[p, :, cols(a)], full.at[p, :, cols(a)], (z_send, z_recv), (a, k), along_z(k)
            )
        if lines > 1:
            for m in range(parts):
                piece = send(
                    full.at[p, :, cols(a, m)], full.at[p, :, cols(a, m)],
                    (x_send, x_recv) if m == 0 else (d_send, d_recv), (a, m, 0), across,
                )
                (from_x if m == 0 else from_d)[a, m, 0] = piece
    for ref in (sl_all, sm_all):
        zero = jnp.zeros(ref.shape[1:], jnp.float32)
        for i in (0, 1, slices + 2, slices + 3):
            ref[i] = zero
    if slices == 1:
        sh_prev[...] = jnp.zeros(sh_prev.shape, jnp.float32)

    count = [0]

    def pass_on(a, view):
        at = (a, count[0])
        count[0] += 1
        landed[a].append(send(view, view, (c_send, c_recv), at, sibling))

    for copy in strains:
        copy.wait_recv()
    x_full[:before] = jnp.where(y > 0, sh_prev[...], 0.0)
    blocks = frames_out.shape[0]

    def frames_part(i):
        fill_products(x_full, frames_out, blocks * i // 3, blocks * (i + 1) // 3)

    frames_part(0)
    for k in range(1, rings):
        low_z[k].wait_recv()
        if lines > 1:
            view = low_all.at[shard(k)]
            low_x[k] = send(view, view, (lx_send, lx_recv), k, across)
    for a, (_, full) in enumerate(arrays):
        count[0] = 0
        for k in range(1, rings):
            from_z[a, k].wait_recv()
            view = full.at[shard(k), :, cols(a)]
            if lines > 1:
                from_x[a, 0, k] = send(view, view, (x_send, x_recv), (a, 0, k), across)
            for m in range(1, parts):
                from_y[a, m, k] = send(view, view, (y_send, y_recv), (a, m, k), along_y(m))
            pass_on(a, view)
    base = count[0]
    frames_part(1)
    for a, (_, full) in enumerate(arrays):
        count[0] = base
        for k in range(rings):
            if lines > 1:
                from_x[a, 0, k].wait_recv()
                view = full.at[shard(k, 1), :, cols(a)]
                if k > 0:
                    for m in range(1, parts):
                        from_d[a, m, k] = send(view, view, (d_send, d_recv), (a, m, k), along_y(m))
                pass_on(a, view)
            for m in range(1, parts):
                if k == 0:
                    continue
                from_y[a, m, k].wait_recv()
                view = full.at[shard(k), :, cols(a, parts - m)]
                pass_on(a, view)
    base = count[0]
    frames_part(2)

    def last_pieces(a, full):
        count[0] = base
        for k in range(rings):
            for m in range(1, parts):
                if lines > 1:
                    from_d[a, m, k].wait_recv()
                    shift = m if k == 0 else parts - m
                    pass_on(a, full.at[shard(k, 1), :, cols(a, shift)])

    low_here, mid_here, low_total, mid_total = bounds(sl_ref, sm_ref, slices)
    taps_low, taps_mid = low_ref.shape[1], mid_ref.shape[1]
    low_chunks, mid_chunks = (r.shape[0] // LANES - 1 for r in (fl_top, fm_top))
    rows_mid = mid_here // LANES

    def low_row(r):
        return sl_all[y + 1 - taps_low // LANES + r]

    def mid_row(r):
        at = r + (y + 2) * rows_mid - taps_mid // LANES - 1
        return sm_all[at // rows_mid, pl.ds(at % rows_mid, 1), :]

    fill_frames(shifted(low_row, HALF_TAPS + 1), fl_top, fl_rest, low_chunks)
    fill_frames(shifted(mid_row, HALF_TAPS), fm_top, fm_rest, mid_chunks)
    for copy in loads[6:]:
        copy.wait()
    last_pieces(*(0, mid_all))
    for copy in low_x.values():
        copy.wait_recv()
    low_w = split(template_filters(low_r, low_all, count_ref[2]))
    parts_low = []
    for c in range(low_chunks):
        at = (low_chunks - 1 - c) * LANES
        parts_low.append(dot3(low_w, (fl_top[at : at + LANES, :LANES], fl_rest[at : at + LANES, :LANES])))
    low = jnp.concatenate(parts_low, axis=1)
    time = y * low_here - (HALF_TAPS + 1) + lax.broadcasted_iota(jnp.int32, low.shape, 1)
    low = jnp.where((time >= 0) & (time < low_total), low, 0.0)
    for copy in landed[0]:
        copy.wait_recv()
    mid_w = split(template_filters(mid_r, mid_all, count_ref[1]))
    last_pieces(*(1, high_all))
    columns = p_full.shape[1]
    lows = [window(low, i) for i in range(-(-columns // WINDOW))]
    for start in range(0, columns, WIDE):
        size_here = min(WIDE, columns - start)
        at = (mid_chunks - taps_mid // LANES - start // LANES) * LANES
        frames = (fm_top[at : at + taps_mid, :size_here], fm_rest[at : at + taps_mid, :size_here])
        value = dot3(mid_w, frames)
        lead = start % WINDOW
        value += one_dot(lows[start // WINDOW], g_out[:, lead : lead + size_here])
        time = y * mid_here - HALF_TAPS + start + lax.broadcasted_iota(jnp.int32, value.shape, 1)
        p_full[:, start : start + size_here] = jnp.where((time >= 0) & (time < mid_total), value, 0.0)
    for i in range(p_out.shape[0]):
        base = i * (WINDOW // RATIO) // LANES * LANES
        p_out[i] = window(p_full[:, base : base + WIDE], i, base)
    for copy in landed[1]:
        copy.wait_recv()
    w = template_filters(high_r, high_all, count_ref[0])
    pieces = [w[:, i : i + WIDE] for i in range(0, w.shape[1], WIDE)]
    for i, (_, summed, _) in enumerate(products(len(pieces))):
        w_out[0, i], w_out[1, i] = split(sum(pieces[k] for k in summed))
    for copy in sent:
        copy.wait_send()


def window(value, i, base=0):
    lead = i * (WINDOW // RATIO) - base
    value = value[:, lead // LANES * LANES :][:, :WIDE]
    lead = lead % LANES
    if lead:
        value = pltpu.roll(value, WIDE - lead, 1)
    top = value.astype(jnp.bfloat16).astype(jnp.float32)
    lane = lax.broadcasted_iota(jnp.int32, value.shape, 1)
    again = jnp.where(lane < 3 * SPAN, pltpu.roll(top, 2 * SPAN, 1), 0.0)
    rest = jnp.where(lane < 2 * SPAN, pltpu.roll(value - top, SPAN, 1), again)
    return jnp.where(lane < SPAN, top, rest).astype(jnp.bfloat16)


def fill_products(x_ref, out_ref, first, last):
    lane = lax.broadcasted_iota(jnp.int32, (LANES, LANES), 1)
    lag = lax.broadcasted_iota(jnp.int32, (LANES, LANES), 0)
    per = WIDE // LANES
    steps = products(math.isqrt(4 ** int(math.log(out_ref.shape[1], 3) + 0.5)))
    blocks = len({k for _, _, outs in steps for k in outs})

    def step(s, _):
        read = {}

        def row(r):
            if r not in read:
                read[r] = x_ref[pl.ds((s + 1) * (blocks * per) + r, 1), :]
            return read[r]

        for i, (offsets, _, _) in enumerate(steps):
            def mixed(e):
                total = 0.0
                for m, c in offsets.items():
                    total = total + row(per * m + e) if c > 0 else total - row(per * m + e)
                return total

            before = staggered(mixed(-per))
            for e in range(1 - per, per):
                now = staggered(mixed(e))
                tile = split(jnp.where(lane >= lag, now, before))
                for a in range(per):
                    if 0 <= a + e < per:
                        for h in range(2):
                            out_ref[s, i, h, a * LANES : (a + 1) * LANES, (a + e) * LANES : (a + e + 1) * LANES] = tile[h]
                before = now
        return 0

    lax.fori_loop(first, last, step, 0)


def bounds(s_low, s_mid, slices):
    low, mid = s_low.shape[0] * LANES, s_mid.shape[0] * LANES
    return low, mid, low * slices, mid * slices


def template_filters(recon_ref, full, count):
    peers, rows, taps = full.shape
    first = (((0,), (0,)), ((), ()))
    index = lax.broadcasted_iota(jnp.int32, recon_ref.shape, 0)
    recon = jnp.where(index < count, recon_ref[...], 0.0)
    if rows % 8 == 0:
        return dot3(split(recon), split(full[...].reshape(peers * rows, taps)), first)
    total = 0.0
    for p in range(peers):
        total += dot3(split(recon[p * rows : (p + 1) * rows]), split(full[p]), first)
    return total


def gather(sizes, count, filters, strains, g, recons):
    low, mid, high = filters
    s_low, s_mid, s_high = strains
    bands, peers, slices = sizes
    lines = 2 if peers % 2 == 0 else 1
    rings = peers // lines
    parts = math.gcd(slices, min(mid.shape[1], high.shape[1]) // (bands * LANES))
    f32, half = jnp.float32, jnp.bfloat16
    basis, _, tmpl = recons[0].shape
    taps_low, taps_mid, taps = (f.shape[1] for f in filters)
    low_here, mid_here, _, _ = bounds(s_low, s_mid, slices)
    samples = s_high.shape[0] * LANES
    columns = mid_here + LANES
    count_products = len(products(taps // WIDE))
    vmem = pl.BlockSpec(memory_space=pltpu.VMEM)
    anywhere = pl.BlockSpec(memory_space=pltpu.HBM)
    dma = pltpu.SemaphoreType.DMA

    def two(*dims):
        return [dma(dims)] * 2

    def frames(rows):
        return [pltpu.VMEM((rows, WIDE), half)] * 2

    held = [pltpu.with_memory_space_constraint(a, pltpu.HBM) for a in (count, *filters, *strains, g, *recons)]
    return pl.pallas_call(
        functools.partial(gather_kernel, (bands, peers, slices, lines, parts)),
        out_shape=[
            pltpu.VMEM((2, count_products, tmpl, WIDE), half),
            pltpu.VMEM((samples // WINDOW, tmpl, WIDE), half),
            pltpu.VMEM(g.shape, half),
            pltpu.VMEM((samples // taps, count_products, 2, WIDE, WIDE), half),
        ],
        in_specs=[pl.BlockSpec(memory_space=pltpu.SMEM)] + [anywhere] * 10,
        out_specs=[vmem] * 4,
        scratch_shapes=[pltpu.VMEM((peers,) + a.shape, f32) for a in filters]
        + [pltpu.VMEM((slices + 4,) + a.shape, f32) for a in (s_low, s_mid)]
        + [pltpu.VMEM((taps // LANES, LANES), f32)]
        + [pltpu.VMEM((basis, tmpl), f32)] * 3
        + [dma((10,)), pltpu.VMEM(((samples + taps) // LANES, LANES), f32)]
        + frames(low_here + 2 * LANES + taps_low) + frames(columns + taps_mid)
        + [pltpu.VMEM((tmpl, columns), f32)]
        + two(3, slices) + two(rings) + two(rings) + two(2, rings)
        + two(2, parts, rings) * 3 + two(2, peers * parts),
        compiler_params=pltpu.CompilerParams(
            collective_id=0, has_side_effects=True, vmem_limit_bytes=28 * 1024 * 1024
        ),
        name="gather_filters",
    )(*held)


def split(value):
    top = value.astype(jnp.bfloat16)
    return top, (value - top.astype(jnp.float32)).astype(jnp.bfloat16)


def one_dot(u, v):
    return lax.dot_general(u, v, (((1,), (0,)), ((), ())), preferred_element_type=jnp.float32)


def dot3(a, b, dims=(((1,), (0,)), ((), ()))):
    def one(u, v):
        return lax.dot_general(u, v, dims, preferred_element_type=jnp.float32)

    return one(a[0], b[0]) + one(a[0], b[1]) + one(a[1], b[0])


def staggered(row):
    return pltpu.roll(jnp.broadcast_to(row, (LANES, LANES)), 0, 1, stride=1, stride_axis=0)


def shifted(read, by):
    lane = lax.broadcasted_iota(jnp.int32, (1, LANES), 1)

    def row(r):
        late = [pltpu.roll(read(r + i), by, 1) for i in range(2)]
        return jnp.where(lane >= by, late[1], late[0])

    return row


def fill_frames(row, top_ref, rest_ref, chunks, first=0, last=None):
    lane = lax.broadcasted_iota(jnp.int32, (LANES, LANES), 1)
    lag = lax.broadcasted_iota(jnp.int32, (LANES, LANES), 0)

    def step(c, before):
        now = staggered(row(c + 1))
        top, rest = split(jnp.where(lane >= lag, now, before))
        left = pl.multiple_of((chunks - 1 - c) * LANES, LANES)
        right = pl.multiple_of((chunks - c) * LANES, LANES)
        for ref, value in ((top_ref, top), (rest_ref, rest)):
            ref[pl.ds(left, LANES), :LANES] = value
            ref[pl.ds(right, LANES), LANES:] = value
        return now

    lax.fori_loop(first, chunks if last is None else last, step, staggered(row(first)))


def compute_kernel(strips, w_ref, p_ref, g_ref, frames_ref, out_ref, tiles, kept, sems):
    rows, count = w_ref.shape[2], w_ref.shape[1]
    depth = rows // strips
    across = tiles.shape[3] // WIDE // 2

    def write(i, q, k):
        half = i % 2
        start = pl.multiple_of((2 * i + q) * (across * WIDE) + k * WIDE, WIDE)
        at = (q * across + k) * WIDE
        return pltpu.make_async_copy(
            tiles.at[half, :, :, pl.ds(at, WIDE)], out_ref.at[:, :, pl.ds(start, WIDE)], sems.at[half, q, k]
        )

    def body(*refs):
        accs = [[refs[(q * 4 + n) * strips : (q * 4 + n + 1) * strips] for n in range(4)] for q in range(2)]

        def part(r):
            return slice(r * depth, (r + 1) * depth)

        def multiply(i, n):
            for q in range(2):
                s = 2 * i + q
                acc = accs[q][n % 4]
                ends = [e for e in (4, 5, 7, 8) if e == n]
                passes = [(frames_ref.at[s, n, 0], (w_ref.at[0, n], w_ref.at[1, n]))]
                passes += [(frames_ref.at[s, n, 1], (w_ref.at[0, n],))]
                if ends:
                    k = ends_at[n]
                    lead = k * WIDE % WINDOW
                    passes += [(g_ref.at[:, lead : lead + WIDE], (p_ref.at[s * (across * WIDE // WINDOW) + k * WIDE // WINDOW],))]
                for step, (right, lefts) in enumerate(passes):
                    staged = (n + step) % 2
                    pltpu.matmul_push_rhs(right[...], staged, q)
                    for turn, left in enumerate(lefts):
                        for r in range(strips):
                            first = staged if turn == 0 and r == 0 else None
                            pltpu.matmul_acc_lhs(acc[r], left[part(r), :], first)

        ends_at = {4: 0, 5: 1, 7: 2, 8: 3}

        def finish(i, n):
            half = i % 2
            for q in range(2):
                for r in range(strips):
                    value = pltpu.matmul_pop(accs[q][n % 4][r])
                    at = (q, slice(None), part(r))
                    if n == 0:
                        kept[q, 0, part(r)] = value
                    elif n in (1, 2):
                        kept[q, n, part(r)] = kept[q, 0, part(r)] + value
                    elif n in (3, 6):
                        kept[q, 3, part(r)] = kept[q, 1, part(r)] + value
                        kept[q, 4, part(r)] = kept[q, 2, part(r)] + value
                    else:
                        k = ends_at[n]
                        at = (q * across + k) * WIDE
                        tiles[half, 0, part(r), at : at + WIDE] = kept[q, 3 + (n - 1) % 3, part(r)] + value
                if n in ends_at:
                    write(i, q, ends_at[n]).start()

        def step(i, _):
            @pl.when(i > 1)
            def _():
                for q in range(2):
                    for k in range(across):
                        write(i - 2, q, k).wait()

            for n in range(count):
                multiply(i, n)
                if n > 0:
                    finish(i, n - 1)
            finish(i, count - 1)
            return 0

        trips = frames_ref.shape[0] // 2
        lax.fori_loop(0, trips, step, 0)
        for i in range(max(0, trips - 2), trips):
            for q in range(2):
                for k in range(across):
                    write(i, q, k).wait()

    specs = []
    for q in range(2):
        specs += [pltpu.ACC(q)((depth, WIDE), jnp.float32)] * (4 * strips)
    pl.run_scoped(body, *specs)


def compute(w, p, g, frames):
    tmpl = w.shape[2]
    blocks = len({k for _, _, outs in products(4) for k in outs})
    samples = frames.shape[0] * blocks * WIDE
    vmem = pl.BlockSpec(memory_space=pltpu.VMEM)
    return pl.pallas_call(
        functools.partial(compute_kernel, max(1, tmpl // 64)),
        out_shape=jax.ShapeDtypeStruct((1, tmpl, samples), jnp.float32),
        in_specs=[vmem] * 4,
        out_specs=pl.BlockSpec(memory_space=pltpu.HBM),
        scratch_shapes=[
            pltpu.VMEM((2, 1, tmpl, 2 * blocks * WIDE), jnp.float32),
            pltpu.VMEM((2, 5, tmpl, WIDE), jnp.float32),
            pltpu.SemaphoreType.DMA((2, 2, blocks)),
        ],
        compiler_params=pltpu.CompilerParams(vmem_limit_bytes=12 * 1024 * 1024),
        name="filter_templates",
    )(w, p, g, frames)


def local(
    sizes, strain_high, strain_mid, strain_low, filters_high, filters_mid, filters_low,
    recon_high, recon_mid, recon_low, basis_count,
):
    g = jnp.asarray(upsample_matrix())
    strains = [s.reshape(-1, LANES) for s in (strain_low, strain_mid, strain_high)]
    out = gather(
        sizes, basis_count, (filters_low, filters_mid, filters_high), strains, g,
        (recon_low, recon_mid, recon_high),
    )
    return compute(*out)


def solution(mesh):
    sizes = tuple(mesh.shape[name] for name in ("band", "tmpl", "tm"))
    in_specs = (
        P("tm"), P("tm"), P("tm"),
        P("tmpl", None), P("tmpl", None), P("tmpl", None),
        P(None, None, "tmpl"), P(None, None, "tmpl"), P(None, None, "tmpl"),
        P(),
    )
    return jax.shard_map(
        functools.partial(local, sizes), mesh=mesh, in_specs=in_specs,
        out_specs=P("band", "tmpl", "tm"), check_vma=False,
    )
```

time: 58.5 us -> 44.8 us (0.77)
  Pallas kernels: 58.1 us -> 44.5 us
    pallas_call x1, Pallas kernels: 22.5 us -> 10.7 us  [compute(): pl.pallas_call(functools.partial(compute_kernel, max(1, tmpl // 64)), out...]
    pallas_call x1, Pallas kernels: 35.6 us -> 33.8 us  [gather(): pl.pallas_call(functools.partial(gather_kernel, (bands, peers, slices, li...]
where the time goes in v1:
time: 44.8 us; the launch traced here: 44.5 us
  Pallas kernels  44.5 us (99%)
    pallas_call x1, Pallas kernels, gather(): pl.pallas_call(functools.partial(gather_kernel, (bands, peers, slices, li...  33.8 us
    pallas_call x1, Pallas kernels, compute(): pl.pallas_call(functools.partial(compute_kernel, max(1, tmpl // 64)), out...  10.7 us

profile of v1, /device:TPU:0, one launch (start us, length us, event | category | flops | bytes accessed | tf_op | source)
XLA Modules:
  0.0 44.5 jit_solution(9738160250444766901)
XLA Ops:
  0.0 33.8 %gather_filters.1 = (bf16[2,9,256,256]{3,2,1,0:T(8,128)(2,1)S(1)}, bf16[16,256,256]{2,1,0:T(8,128)(2,1)S(1)}, bf16[256,512]{1,0:T(8,128)(2,1)S(1)}, bf16[8,9,2,256,256]{4,3,2,1,0:T(8,128)(2,1)S(1)}) custom-call(s32[3]{0:T(128)} %count_ref.1, f32[40,128]{1,0:T(8,128)} %low_ref.1, f32[40,1024]{1,0:T(8,128)} %mid_ref.1, f32[40,1024]{1,0:T(8,128)} %high_ref.1, ...), custom_call_target="tpu_custom_call" | custom-call | tf_op jit(solution)/shard_map/gather_filters/pallas_call | solution.py:363
  33.8 10.7 %filter_templates.1 = f32[1,256,8192]{2,1,0:T(8,128)} custom-call(bf16[2,9,256,256]{3,2,1,0:T(8,128)(2,1)S(1)} %get-tuple-element.9.w_ref, bf16[16,256,256]{2,1,0:T(8,128)(2,1)S(1)} %get-tuple-element.10.p_ref, bf16[256,512]{1,0:T(8,128)(2,1)S(1)} %get-tuple-element.11.g_ref, bf16[8,9,2,256,256]{4,3,2,1,0:T(8,128)(2,1)S(1)} %get-tuple-element.12.frames_ref), custom_call_target="tpu_custom_call" | custom-call | tf_op jit(solution)/shard_map/filter_templates/pallas_call | solution.py:528

commit v2 on v1

v2 whole, which is shorter than its diff:
```python
import functools
import math

import jax
import jax.numpy as jnp
import numpy as np
from jax import lax
from jax.experimental import pallas as pl
from jax.experimental.pallas import tpu as pltpu
from jax.sharding import PartitionSpec as P

RATIO = 8
HALF_TAPS = 8
LANES = 128
WIDE = 256
WINDOW = 2 * WIDE
SPAN = WINDOW // RATIO + 2 * HALF_TAPS
MESH = pl.DeviceIdType.MESH


def upsample_matrix():
    u = np.arange(SPAN)[:, None]
    v = np.arange(WINDOW)[None, :]
    lag = u - v // RATIO
    offset = (v % RATIO) / RATIO - (lag - HALF_TAPS)
    value = np.sinc(offset) * (0.5 + 0.5 * np.cos(np.pi * offset / (HALF_TAPS + 1)))
    value = np.where((lag >= 0) & (lag < 2 * HALF_TAPS), value, 0.0).astype(np.float32)
    top = value.astype(jnp.bfloat16)
    rest = (value - top.astype(np.float32)).astype(jnp.bfloat16)
    pad = np.zeros((WIDE - 3 * SPAN, WINDOW), jnp.bfloat16)
    return np.concatenate([top, top, rest, pad], axis=0)


def products(blocks):
    if blocks == 1:
        return [({0: 1}, (0,), (0,))]
    n = blocks // 2
    inner = products(n)

    def less(frames, shift):
        total = dict(frames)
        total = {m: -c for m, c in frames.items()}
        for m, c in frames.items():
            total[m + shift] = total.get(m + shift, 0) + c
        return {m: c for m, c in total.items() if c}

    both = [(f, w + tuple(i + n for i in w), o + tuple(k + n for k in o)) for f, w, o in inner]
    first = [(less(f, -n), tuple(i + n for i in w), o) for f, w, o in inner]
    last = [(less(f, n), w, tuple(k + n for k in o)) for f, w, o in inner]
    return both + first + last


def gather_kernel(
    sizes, count_ref, low_ref, mid_ref, high_ref, sl_ref, sm_ref, sh_ref, g_ref,
    recon_low, recon_mid, recon_high,
    w_out, p_full, g_out, frames_out,
    low_all, mid_all, high_all, sl_all, sm_all, sh_prev,
    low_r, mid_r, high_r, low_l, mid_l, high_l, load_sem, x_full,
    fl_top, fl_rest, fm_top, fm_rest, wm_top, wm_rest, lows, w_full,
    strain_send, strain_recv, lo_send, lf_send, lz_recv, lx_send, lx_recv, lc_send, lc_recv,
    zo_send, zf_send, z_recv, x_send, x_recv, y_send, y_recv, d_send, d_recv, c_send, c_recv,
):
    bands, peers, slices, lines, parts = sizes
    rings = peers // lines
    b, p, y = lax.axis_index("band"), lax.axis_index("tmpl"), lax.axis_index("tm")
    z, x = p // lines, p % lines
    part = y % parts

    def at_level(level):
        return (b, ((level + rings) % rings) * lines + x, y)

    def on_line(level):
        return (level >= 0) & (level < rings)

    def along_y(m):
        return (b, p, y - part + (part + m) % parts)

    across = (b, z * lines + (x + 1) % lines, y)
    sibling = (1 - b, p, y)
    before = sh_prev.shape[0]
    loads = []
    for i, (src, dst) in enumerate((
        (low_ref, low_all.at[p]), (mid_ref, mid_all.at[p]), (high_ref, high_all.at[p]),
        (sl_ref, sl_all.at[2 + y]), (sm_ref, sm_all.at[2 + y]),
        (sh_ref, x_full.at[pl.ds(before, sh_ref.shape[0])]),
        (recon_low.at[:, b, :], low_r), (recon_mid.at[:, b, :], mid_r), (recon_high.at[:, b, :], high_r),
        (g_ref, g_out),
    )):
        copy = pltpu.make_async_copy(src, dst, load_sem.at[i])
        copy.start()
        loads.append(copy)

    reach = [1, -1] if rings > 1 else []
    barrier = pltpu.get_barrier_semaphore()

    def greet(device):
        pl.semaphore_signal(barrier, inc=1, device_id=device, device_id_type=MESH)

    others = [sibling] + [(b, p, (y + k) % slices) for k in range(1, slices)]
    if lines > 1:
        others += [across]
    for device in others:
        greet(device)
    waiting = len(others)
    for step in reach:
        pl.when(on_line(z + step))(functools.partial(greet, at_level(z + step)))
        waiting = waiting + jnp.where(on_line(z + step), 1, 0)
    pl.semaphore_wait(barrier, waiting)
    for copy in loads[:6]:
        copy.wait()

    sent = []

    def remote(view, out, into, device):
        return pltpu.make_async_remote_copy(
            src_ref=view, dst_ref=view, send_sem=out, recv_sem=into, device_id=device, device_id_type=MESH
        )

    def send(view, out, into, device, when=None):
        copy = remote(view, out, into, device)
        if when is None:
            copy.start()
        else:
            pl.when(when)(copy.start)
        sent.append((copy, when))

    def arrived(view, out, into, when=None):
        copy = remote(view, out, into, sibling)
        if when is None:
            copy.wait_recv()
        else:
            pl.when(when)(copy.wait_recv)

    near = jnp.minimum(z, rings - 1 - z)
    longer = jnp.where(z < rings - 1 - z, 1, -1)
    levels = [(z, 0)]
    for n in range(1, rings):
        inside = n <= 2 * near
        step = jnp.where(inside, 1 - 2 * (n % 2), longer)
        d = jnp.where(inside, (n + 1) // 2, n - near)
        levels.append((z + step * d, step))

    arrays = (mid_all, high_all)
    size = [ref.shape[2] // (bands * parts) for ref in arrays]

    def cols(a, m=0, band=b):
        start = (band * parts + (part + m) % parts) * size[a]
        return pl.ds(pl.multiple_of(start, LANES), size[a])

    def piece(a, n, other=0, m=0, band=b):
        return arrays[a].at[levels[n][0] * lines + (x + other) % lines, :, cols(a, m, band)]

    mine = x % bands == b

    def low(n, other=0):
        return low_all.at[levels[n][0] * lines + (x + other) % lines]

    def own_low():
        for i, step in enumerate(reach):
            send(low(0), lo_send.at[i], lz_recv.at[z], at_level(z + step), mine & on_line(z + step))
        if lines > 1:
            send(low(0), lx_send.at[z], lx_recv.at[z], across, mine)

    def own_z(a):
        for i, step in enumerate(reach):
            send(piece(a, 0), zo_send.at[a, i], z_recv.at[a, z], at_level(z + step), on_line(z + step))

    def own_x(a, m):
        if lines > 1:
            send(piece(a, 0, 0, m), x_send.at[a, m, z], x_recv.at[a, m, z], across)

    def low_from_z(n):
        level, step = levels[n]
        ahead = z - step
        arrived(low(n), lf_send.at[level], lz_recv.at[level], mine)
        send(low(n), lf_send.at[level], lz_recv.at[level], at_level(ahead), mine & on_line(ahead))
        if lines > 1:
            send(low(n), lx_send.at[level], lx_recv.at[level], across, mine)
        send(low(n), lc_send.at[0, level], lc_recv.at[0, level], sibling, mine)

    def low_from_x(n):
        if lines > 1:
            level = levels[n][0]
            arrived(low(n, 1), lx_send.at[level], lx_recv.at[level], jnp.logical_not(mine))
            send(low(n, 1), lc_send.at[1, level], lc_recv.at[1, level], sibling, jnp.logical_not(mine))

    def low_landed():
        for n in range(rings):
            level = levels[n][0]
            if n > 0:
                arrived(low(n), lc_send.at[0, level], lc_recv.at[0, level], jnp.logical_not(mine))
            if lines > 1:
                arrived(low(n, 1), lc_send.at[1, level], lc_recv.at[1, level], mine)

    def pass_on(a, line, n, m, view):
        level = levels[n][0]
        send(view, c_send.at[a, line, m, level], c_recv.at[a, line, m, level], sibling)

    def from_z(a, n):
        level, step = levels[n]
        ahead = z - step
        view = piece(a, n)
        arrived(view, zf_send.at[a, level], z_recv.at[a, level])
        send(view, zf_send.at[a, level], z_recv.at[a, level], at_level(ahead), on_line(ahead))
        if lines > 1:
            send(view, x_send.at[a, 0, level], x_recv.at[a, 0, level], across)
        for m in range(1, parts):
            send(view, y_send.at[a, m, level], y_recv.at[a, m, level], along_y(m))
        pass_on(a, 0, n, 0, view)

    def from_x(a, n, m=0):
        if lines > 1:
            level = levels[n][0]
            view = piece(a, n, 1, m)
            arrived(view, x_send.at[a, m, level], x_recv.at[a, m, level])
            if n > 0:
                for k in range(1, parts):
                    send(view, d_send.at[a, k, level], d_recv.at[a, k, level], along_y(k))
            pass_on(a, 1, n, m, view)

    def from_y(a, n):
        level = levels[n][0]
        for m in range(1, parts):
            view = piece(a, n, 0, parts - m)
            arrived(view, y_send.at[a, m, level], y_recv.at[a, m, level])
            pass_on(a, 0, n, m, view)

    def from_xy(a, n):
        if lines > 1:
            level = levels[n][0]
            for m in range(1, parts):
                view = piece(a, n, 1, parts - m)
                arrived(view, d_send.at[a, m, level], d_recv.at[a, m, level])
                pass_on(a, 1, n, m, view)

    def landed(a, own):
        for n in range(rings):
            level = levels[n][0]
            for m in range(1) if own else range(1, parts):
                if n > 0:
                    view = piece(a, n, 0, (parts - m) % parts, 1 - b)
                    arrived(view, c_send.at[a, 0, m, level], c_recv.at[a, 0, m, level])
                if lines > 1:
                    view = piece(a, n, 1, m if n == 0 else (parts - m) % parts, 1 - b)
                    arrived(view, c_send.at[a, 1, m, level], c_recv.at[a, 1, m, level])

    def blocks(a, own):
        parted = range(1) if own else range(1, parts)
        return [(cols(a, m, band), (band * parts + (part + m) % parts) * size[a]) for m in parted for band in range(bands)]

    strains = []
    for k in range(1, slices):
        device = (b, p, (y + k) % slices)
        for i, ref in enumerate((sl_all, sm_all)):
            send(ref.at[2 + y], strain_send.at[i, k], strain_recv.at[i, k], device)
            strains.append((ref.at[2 + (y + slices - k) % slices], strain_send.at[i, k], strain_recv.at[i, k]))
    if slices > 1:
        tail = pl.ds(x_full.shape[0] - before, before)
        copy = pltpu.make_async_remote_copy(
            src_ref=x_full.at[tail], dst_ref=sh_prev, send_sem=strain_send.at[2, 0], recv_sem=strain_recv.at[2, 0],
            device_id=(b, p, (y + 1) % slices), device_id_type=MESH,
        )
        copy.start()
        sent.append((copy, None))

    own_low()
    for a in range(2):
        own_z(a)
        own_x(a, 0)
    for a in range(2):
        for m in range(1, parts):
            own_x(a, m)

    low_here, mid_here, low_total, mid_total = bounds(sl_ref, sm_ref, slices)
    taps_low, taps_mid = low_ref.shape[1], mid_ref.shape[1]
    low_chunks, mid_chunks = (r.shape[0] // LANES - 1 for r in (fl_top, fm_top))
    rows_mid = mid_here // LANES
    columns = p_full.shape[1]

    def low_row(r):
        return sl_all[y + 1 - taps_low // LANES + r]

    def mid_row(r):
        at = r + (y + 2) * rows_mid - taps_mid // LANES - 1
        return sm_all[at // rows_mid, pl.ds(at % rows_mid, 1), :]

    recons = ((low_r, low_l), (mid_r, mid_l), (high_r, high_l))

    def prepare(i):
        loads[6 + i].wait()
        spread_recon(*recons[i], count_ref[2 - i])

    work = [functools.partial(fill_frames, shifted(low_row, HALF_TAPS + 1), fl_top, fl_rest, low_chunks, 0, low_chunks)]
    for first in range(0, mid_chunks, 3):
        last = min(mid_chunks, first + 3)
        work += [functools.partial(fill_frames, shifted(mid_row, HALF_TAPS), fm_top, fm_rest, mid_chunks, first, last)]
    total = frames_out.shape[1]
    for block in range(frames_out.shape[0]):
        for first, last in ((0, total // 2 + 1), (total // 2 + 1, total)):
            work += [functools.partial(fill_products, x_full, frames_out, block, first, last)]

    def spend(count):
        for _ in range(count):
            if work:
                work.pop(0)()

    others = range(1, rings)
    prepare(0)
    prepare(1)
    prepare(2)
    loads[9].wait()
    for ref in (sl_all, sm_all):
        zero = jnp.zeros(ref.shape[1:], jnp.float32)
        for i in (0, 1, slices + 2, slices + 3):
            ref[i] = zero
    if slices == 1:
        sh_prev[...] = jnp.zeros(sh_prev.shape, jnp.float32)
    else:
        copy.wait_recv()
    for view in strains:
        arrived(*view)
    x_full[:before] = jnp.where(y > 0, sh_prev[...], 0.0)
    spend(1)
    starts = range(0, columns, WIDE)

    def mid_tile(start, own):
        size_here = min(WIDE, columns - start)
        at = (mid_chunks - taps_mid // LANES - start // LANES) * LANES
        tile = slice(start, start + size_here)
        value = 0.0 if own else p_full[:, tile]
        for lanes, first in blocks(0, own):
            rows = pl.ds(pl.multiple_of(at + first, LANES), size[0])
            value += dot3((wm_top[:, lanes], wm_rest[:, lanes]), (fm_top[rows, :size_here], fm_rest[rows, :size_here]))
        if own:
            lead = start % WINDOW
            value += one_dot(lows[start // WINDOW], g_out[:, lead : lead + size_here])
        else:
            time = y * mid_here - HALF_TAPS + start + lax.broadcasted_iota(jnp.int32, value.shape, 1)
            value = jnp.where((time >= 0) & (time < mid_total), value, 0.0)
        p_full[:, tile] = value

    def mid_filters(own):
        for lanes, _ in blocks(0, own):
            wm_top[:, lanes], wm_rest[:, lanes] = split(template_filters(mid_r, mid_l, mid_all, lanes, count_ref[1]))

    def high_filters(own):
        for lanes, _ in blocks(1, own):
            w_full[:, lanes] = template_filters(high_r, high_l, high_all, lanes, count_ref[0])

    def low_part():
        low_w = split(template_filters(low_r, low_l, low_all, slice(None), count_ref[2]))
        parts_low = []
        for c in range(low_chunks):
            at = (low_chunks - 1 - c) * LANES
            parts_low.append(dot3(low_w, (fl_top[at : at + LANES, :LANES], fl_rest[at : at + LANES, :LANES])))
        value = jnp.concatenate(parts_low, axis=1)
        time = y * low_here - (HALF_TAPS + 1) + lax.broadcasted_iota(jnp.int32, value.shape, 1)
        value = jnp.where((time >= 0) & (time < low_total), value, 0.0)
        for i in range(lows.shape[0]):
            lows[i] = window(value, i * (WINDOW // RATIO))

    for a in range(2):
        for n in others[:2]:
            from_z(a, n)
    for n in others[:2]:
        low_from_z(n)
    spend(3)
    for n in others[2:]:
        from_z(0, n)
        low_from_z(n)
        from_z(1, n)
    spend(1)
    for n in others[:2]:
        from_x(0, n)
    spend(1)
    for n in range(rings):
        low_from_x(n)
    from_x(0, 0)
    spend(1)
    for n in others[2:]:
        from_x(0, n)
    for m in range(1, parts):
        from_x(0, 0, m)
    spend(1)
    low_landed()
    low_part()
    for n in others[:2]:
        from_x(1, n)
    landed(0, True)
    mid_filters(True)
    for n in others[:2]:
        from_y(0, n)
    steps = [functools.partial(from_x, 1, n) for n in others[2:]]
    steps += [functools.partial(from_y, 0, n) for n in others[2:]]
    steps += [functools.partial(from_xy, 0, n) for n in others]
    steps += [functools.partial(from_x, 1, 0)]
    for start in starts:
        mid_tile(start, True)
        if steps:
            steps.pop(0)()
        spend(1)
    for step in steps:
        step()
        spend(1)
    for n in others:
        from_y(1, n)
    spend(3)
    for m in range(1, parts):
        from_x(1, 0, m)
    landed(1, True)
    high_filters(True)
    spend(2)
    landed(0, False)
    mid_filters(False)
    later = list(others)
    for start in starts:
        mid_tile(start, False)
        if later:
            from_xy(1, later.pop(0))
    for n in later:
        from_xy(1, n)
    spend(len(work))
    landed(1, False)
    high_filters(False)
    pieces = [w_full[:, i : i + WIDE] for i in range(0, w_full.shape[1], WIDE)]
    for i, (_, summed, _) in enumerate(products(len(pieces))):
        w_out[0, i], w_out[1, i] = split(sum(pieces[k] for k in summed))
    for copy, when in sent:
        if when is None:
            copy.wait_send()
        else:
            pl.when(when)(copy.wait_send)


def spread_recon(recon_ref, out_ref, count):
    index = lax.broadcasted_iota(jnp.int32, recon_ref.shape, 0)
    top, rest = split(jnp.where(index < count, recon_ref[...], 0.0).T)
    out_ref[...] = jnp.concatenate([top, rest, top], axis=1)


def window(value, lead):
    value = value[:, lead // LANES * LANES :][:, :WIDE]
    lead = lead % LANES
    if lead:
        value = pltpu.roll(value, WIDE - lead, 1)
    top = value.astype(jnp.bfloat16).astype(jnp.float32)
    lane = lax.broadcasted_iota(jnp.int32, value.shape, 1)
    again = jnp.where(lane < 3 * SPAN, pltpu.roll(top, 2 * SPAN, 1), 0.0)
    rest = jnp.where(lane < 2 * SPAN, pltpu.roll(value - top, SPAN, 1), again)
    return jnp.where(lane < SPAN, top, rest).astype(jnp.bfloat16)


def fill_products(x_ref, out_ref, block, first, last):
    lane = lax.broadcasted_iota(jnp.int32, (LANES, LANES), 1)
    lag = lax.broadcasted_iota(jnp.int32, (LANES, LANES), 0)
    per = WIDE // LANES
    steps = products(2 ** round(math.log(out_ref.shape[1], 3)))
    start = (block + 1) * per * len({k for _, _, outs in steps for k in outs})
    for i, (offsets, _, _) in list(enumerate(steps))[first:last]:
        before = None
        for e in range(-per, per):
            mixed = 0.0
            for m, c in offsets.items():
                row = x_ref[start + per * m + e : start + per * m + e + 1, :]
                mixed = mixed + row if c > 0 else mixed - row
            now = staggered(mixed)
            if before is not None:
                tile = split(jnp.where(lane >= lag, now, before))
                for a in range(max(0, -e), min(per, per - e)):
                    for h in range(2):
                        out_ref[block, i, h, a * LANES : (a + 1) * LANES, (a + e) * LANES : (a + e + 1) * LANES] = tile[h]
            before = now


def bounds(s_low, s_mid, slices):
    low, mid = s_low.shape[0] * LANES, s_mid.shape[0] * LANES
    return low, mid, low * slices, mid * slices


def template_filters(recon_ref, spread_ref, full, lanes, count):
    peers, rows, _ = full.shape
    if rows % 8 == 0:
        filters = full[:, :, lanes]
        top, rest = split(filters.reshape(peers * rows, filters.shape[2]))
        return one_dot(spread_ref[...], jnp.concatenate([top, top, rest], axis=0))
    first = (((0,), (0,)), ((), ()))
    index = lax.broadcasted_iota(jnp.int32, recon_ref.shape, 0)
    recon = jnp.where(index < count, recon_ref[...], 0.0)
    total = 0.0
    for p in range(peers):
        total += dot3(split(recon[p * rows : (p + 1) * rows]), split(full[p, :, lanes]), first)
    return total


def gather(sizes, count, filters, strains, g, recons):
    low, mid, high = filters
    s_low, s_mid, s_high = strains
    bands, peers, slices = sizes
    lines = 2 if peers % 2 == 0 else 1
    rings = peers // lines
    parts = math.gcd(slices, min(mid.shape[1], high.shape[1]) // (bands * LANES))
    f32, half = jnp.float32, jnp.bfloat16
    basis, _, tmpl = recons[0].shape
    taps_low, taps_mid, taps = (f.shape[1] for f in filters)
    low_here, mid_here, _, _ = bounds(s_low, s_mid, slices)
    samples = s_high.shape[0] * LANES
    columns = mid_here + LANES
    count_products = len(products(taps // WIDE))
    vmem = pl.BlockSpec(memory_space=pltpu.VMEM)
    anywhere = pl.BlockSpec(memory_space=pltpu.HBM)
    dma = pltpu.SemaphoreType.DMA

    def two(*dims):
        return [dma(dims)] * 2

    def frames(rows):
        return [pltpu.VMEM((rows, WIDE), half)] * 2

    held = [pltpu.with_memory_space_constraint(a, pltpu.HBM) for a in (count, *filters, *strains, g, *recons)]
    return pl.pallas_call(
        functools.partial(gather_kernel, (bands, peers, slices, lines, parts)),
        out_shape=[
            pltpu.VMEM((2, count_products, tmpl, WIDE), half),
            pltpu.VMEM((tmpl, columns), f32),
            pltpu.VMEM(g.shape, half),
            pltpu.VMEM((samples // taps, count_products, 2, WIDE, WIDE), half),
        ],
        in_specs=[pl.BlockSpec(memory_space=pltpu.SMEM)] + [anywhere] * 10,
        out_specs=[vmem] * 4,
        scratch_shapes=[pltpu.VMEM((peers,) + a.shape, f32) for a in filters]
        + [pltpu.VMEM((slices + 4,) + a.shape, f32) for a in (s_low, s_mid)]
        + [pltpu.VMEM((taps // LANES, LANES), f32)]
        + [pltpu.VMEM((basis, tmpl), f32)] * 3 + [pltpu.VMEM((tmpl, 3 * basis), half)] * 3
        + [dma((10,)), pltpu.VMEM(((samples + taps) // LANES, LANES), f32)]
        + frames(low_here + 2 * LANES + taps_low) + frames(columns + taps_mid)
        + [pltpu.VMEM((tmpl, taps_mid), half)] * 2
        + [pltpu.VMEM((-(-columns // WINDOW), tmpl, WIDE), half), pltpu.VMEM((tmpl, taps), f32)]
        + two(3, slices) + [dma((2,)), dma((rings,)), dma((rings,))] + two(rings) + two(2, rings)
        + [dma((2, 2)), dma((2, rings)), dma((2, rings))]
        + two(2, parts, rings) * 3 + two(2, 2, parts, rings),
        compiler_params=pltpu.CompilerParams(
            collective_id=0, has_side_effects=True, vmem_limit_bytes=28 * 1024 * 1024
        ),
        name="gather_filters",
    )(*held)


def split(value):
    top = value.astype(jnp.bfloat16)
    return top, (value - top.astype(jnp.float32)).astype(jnp.bfloat16)


def one_dot(u, v):
    return lax.dot_general(u, v, (((1,), (0,)), ((), ())), preferred_element_type=jnp.float32)


def dot3(a, b, dims=(((1,), (0,)), ((), ()))):
    def one(u, v):
        return lax.dot_general(u, v, dims, preferred_element_type=jnp.float32)

    return one(a[0], b[0]) + one(a[0], b[1]) + one(a[1], b[0])


def staggered(row):
    return pltpu.roll(jnp.broadcast_to(row, (LANES, LANES)), 0, 1, stride=1, stride_axis=0)


def shifted(read, by):
    lane = lax.broadcasted_iota(jnp.int32, (1, LANES), 1)

    def row(r):
        late = [pltpu.roll(read(r + i), by, 1) for i in range(2)]
        return jnp.where(lane >= by, late[1], late[0])

    return row


def fill_frames(row, top_ref, rest_ref, chunks, first, last):
    lane = lax.broadcasted_iota(jnp.int32, (LANES, LANES), 1)
    lag = lax.broadcasted_iota(jnp.int32, (LANES, LANES), 0)
    before = staggered(row(first))
    for c in range(first, last):
        now = staggered(row(c + 1))
        top, rest = split(jnp.where(lane >= lag, now, before))
        left, right = (chunks - 1 - c) * LANES, (chunks - c) * LANES
        for ref, value in ((top_ref, top), (rest_ref, rest)):
            ref[left : left + LANES, :LANES] = value
            ref[right : right + LANES, LANES:] = value
        before = now


def compute_kernel(strips, w_ref, p_ref, g_ref, frames_ref, out_ref, tiles, kept, spread, sems):
    rows, count = w_ref.shape[2], w_ref.shape[1]
    depth = rows // strips
    across = tiles.shape[3] // WIDE // 2

    def write(i, q, k):
        half = i % 2
        start = pl.multiple_of((2 * i + q) * (across * WIDE) + k * WIDE, WIDE)
        at = (q * across + k) * WIDE
        return pltpu.make_async_copy(
            tiles.at[half, :, :, pl.ds(at, WIDE)], out_ref.at[:, :, pl.ds(start, WIDE)], sems.at[half, q, k]
        )

    def body(*refs):
        accs = [[refs[(q * 4 + n) * strips : (q * 4 + n + 1) * strips] for n in range(4)] for q in range(2)]

        def part(r):
            return slice(r * depth, (r + 1) * depth)

        def multiply(i, n):
            for q in range(2):
                s = 2 * i + q
                acc = accs[q][n % 4]
                ends = [e for e in (4, 5, 7, 8) if e == n]
                passes = [(frames_ref.at[s, n, 0], (w_ref.at[0, n], w_ref.at[1, n]))]
                passes += [(frames_ref.at[s, n, 1], (w_ref.at[0, n],))]
                if ends:
                    k = ends_at[n]
                    lead = k * WIDE % WINDOW
                    passes += [(g_ref.at[:, lead : lead + WIDE], (spread.at[(q * across + k) * WIDE // WINDOW],))]
                for step, (right, lefts) in enumerate(passes):
                    staged = (n + step) % 2
                    pltpu.matmul_push_rhs(right[...], staged, q)
                    for turn, left in enumerate(lefts):
                        for r in range(strips):
                            first = staged if turn == 0 and r == 0 else None
                            pltpu.matmul_acc_lhs(acc[r], left[part(r), :], first)

        ends_at = {4: 0, 5: 1, 7: 2, 8: 3}

        def finish(i, n):
            half = i % 2
            for q in range(2):
                for r in range(strips):
                    value = pltpu.matmul_pop(accs[q][n % 4][r])
                    at = (q, slice(None), part(r))
                    if n == 0:
                        kept[q, 0, part(r)] = value
                    elif n in (1, 2):
                        kept[q, n, part(r)] = kept[q, 0, part(r)] + value
                    elif n in (3, 6):
                        kept[q, 3, part(r)] = kept[q, 1, part(r)] + value
                        kept[q, 4, part(r)] = kept[q, 2, part(r)] + value
                    else:
                        k = ends_at[n]
                        at = (q * across + k) * WIDE
                        tiles[half, 0, part(r), at : at + WIDE] = kept[q, 3 + (n - 1) % 3, part(r)] + value
                if n in ends_at:
                    write(i, q, ends_at[n]).start()

        def step(i, _):
            @pl.when(i > 1)
            def _():
                for q in range(2):
                    for k in range(across):
                        write(i - 2, q, k).wait()

            stride = WINDOW // RATIO
            span = spread.shape[0] * stride
            for j in range(spread.shape[0]):
                lead = j * stride % LANES
                base = pl.multiple_of(i * span + j * stride // LANES * LANES, LANES)
                for r in range(strips):
                    spread[j, part(r)] = window(p_ref[part(r), pl.ds(base, WIDE)], lead)
            for n in range(count):
                multiply(i, n)
                if n > 0:
                    finish(i, n - 1)
            finish(i, count - 1)
            return 0

        trips = frames_ref.shape[0] // 2
        lax.fori_loop(0, trips, step, 0)
        for i in range(max(0, trips - 2), trips):
            for q in range(2):
                for k in range(across):
                    write(i, q, k).wait()

    specs = []
    for q in range(2):
        specs += [pltpu.ACC(q)((depth, WIDE), jnp.float32)] * (4 * strips)
    pl.run_scoped(body, *specs)


def compute(w, p, g, frames):
    tmpl = w.shape[2]
    blocks = len({k for _, _, outs in products(4) for k in outs})
    samples = frames.shape[0] * blocks * WIDE
    vmem = pl.BlockSpec(memory_space=pltpu.VMEM)
    return pl.pallas_call(
        functools.partial(compute_kernel, max(1, tmpl // 64)),
        out_shape=jax.ShapeDtypeStruct((1, tmpl, samples), jnp.float32),
        in_specs=[vmem] * 4,
        out_specs=pl.BlockSpec(memory_space=pltpu.HBM),
        scratch_shapes=[
            pltpu.VMEM((2, 1, tmpl, 2 * blocks * WIDE), jnp.float32),
            pltpu.VMEM((2, 5, tmpl, WIDE), jnp.float32),
            pltpu.VMEM((2 * blocks * WIDE // WINDOW, tmpl, WIDE), jnp.bfloat16),
            pltpu.SemaphoreType.DMA((2, 2, blocks)),
        ],
        compiler_params=pltpu.CompilerParams(vmem_limit_bytes=12 * 1024 * 1024),
        name="filter_templates",
    )(w, p, g, frames)


def local(
    sizes, strain_high, strain_mid, strain_low, filters_high, filters_mid, filters_low,
    recon_high, recon_mid, recon_low, basis_count,
):
    g = jnp.asarray(upsample_matrix())
    strains = [s.reshape(-1, LANES) for s in (strain_low, strain_mid, strain_high)]
    out = gather(
        sizes, basis_count, (filters_low, filters_mid, filters_high), strains, g,
        (recon_low, recon_mid, recon_high),
    )
    return compute(*out)


def solution(mesh):
    sizes = tuple(mesh.shape[name] for name in ("band", "tmpl", "tm"))
    in_specs = (
        P("tm"), P("tm"), P("tm"),
        P("tmpl", None), P("tmpl", None), P("tmpl", None),
        P(None, None, "tmpl"), P(None, None, "tmpl"), P(None, None, "tmpl"),
        P(),
    )
    return jax.shard_map(
        functools.partial(local, sizes), mesh=mesh, in_specs=in_specs,
        out_specs=P("band", "tmpl", "tm"), check_vma=False,
    )
```

time: 44.8 us -> 42.2 us (0.942)
  Pallas kernels: 44.5 us -> 42.1 us
    pallas_call x1, Pallas kernels: 33.8 us -> 31.1 us  [gather(): pl.pallas_call(functools.partial(gather_kernel, (bands, peers, slices, li...]
where the time goes in v2:
time: 42.2 us; the launch traced here: 42.1 us
  Pallas kernels  42.1 us (100%)
    pallas_call x1, Pallas kernels, gather(): pl.pallas_call(functools.partial(gather_kernel, (bands, peers, slices, li...  31.1 us
    pallas_call x1, Pallas kernels, compute(): pl.pallas_call(functools.partial(compute_kernel, max(1, tmpl // 64)), out...  10.9 us

profile of v2, /device:TPU:0, one launch (start us, length us, event | category | flops | bytes accessed | tf_op | source)
XLA Modules:
  0.0 42.1 jit_solution(4390546812266220859)
XLA Ops:
  0.0 31.1 %gather_filters.1 = (bf16[2,9,256,256]{3,2,1,0:T(8,128)(2,1)S(1)}, f32[256,1152]{1,0:T(8,128)S(1)}, bf16[256,512]{1,0:T(8,128)(2,1)S(1)}, bf16[8,9,2,256,256]{4,3,2,1,0:T(8,128)(2,1)S(1)}) custom-call(s32[3]{0:T(128)} %count_ref.1, f32[40,128]{1,0:T(8,128)} %low_ref.1, f32[40,1024]{1,0:T(8,128)} %mid_ref.1, f32[40,1024]{1,0:T(8,128)} %high_ref.1, ...), custom_call_target="tpu_custom_call" | custom-call | tf_op jit(solution)/shard_map/gather_filters/pallas_call | solution.py:520
  31.1 10.9 %filter_templates.1 = f32[1,256,8192]{2,1,0:T(8,128)} custom-call(bf16[2,9,256,256]{3,2,1,0:T(8,128)(2,1)S(1)} %get-tuple-element.9.w_ref, f32[256,1152]{1,0:T(8,128)S(1)} %get-tuple-element.10.p_ref, bf16[256,512]{1,0:T(8,128)(2,1)S(1)} %get-tuple-element.11.g_ref, bf16[8,9,2,256,256]{4,3,2,1,0:T(8,128)(2,1)S(1)} %get-tuple-element.12.frames_ref), custom_call_target="tpu_custom_call" | custom-call | tf_op jit(solution)/shard_map/filter_templates/pallas_call | solution.py:691

commit v3 on v2

--- a/solution.py
+++ b/solution.py
@@ -16,6 +16,15 @@
 WINDOW = 2 * WIDE
 SPAN = WINDOW // RATIO + 2 * HALF_TAPS
 MESH = pl.DeviceIdType.MESH
+ORDER = (
+    ("f", 2), ("z", 0, 1), ("z", 0, 2), ("f", 2), ("x", 0, 0), ("f", 1), ("z", 1, 1), ("z", 1, 2), ("f", 5),
+    ("b", 1, 0), ("z", 0, 3), ("f", 1), ("y", 0, 1), ("f", 1), ("x", 0, 1), ("f", 1), ("z", 1, 3), ("f", 1),
+    ("y", 0, 2), ("y", 1, 1), ("x", 0, 2), ("x", 1, 0), ("f", 1), ("b", 0, 0), ("x", 1, 1), ("f", 1), ("y", 1, 2),
+    ("f", 1), ("x", 0, 3), ("l",), ("y", 0, 3), ("f", 2), ("x", 1, 3), ("d", 0, 1), ("m", 1), ("x", 1, 2), ("t", 1),
+    ("t", 1), ("d", 0, 2), ("f", 2), ("y", 1, 3), ("d", 0, 3), ("f", 1), ("t", 1), ("t", 1), ("d", 1, 1), ("t", 1),
+    ("d", 1, 3), ("m", 0), ("t", 0), ("t", 0), ("d", 1, 2), ("t", 0), ("t", 0), ("h", 1), ("t", 0), ("f", 1),
+)
+LATE_X = ((0, 2), (1, 1))
 
 
 def upsample_matrix():
@@ -213,7 +222,7 @@
             level = levels[n][0]
             view = piece(a, n, 1, m)
             arrived(view, x_send.at[a, m, level], x_recv.at[a, m, level])
-            if n > 0:
+            if n > 0 and (a, n) not in LATE_X:
                 for k in range(1, parts):
                     send(view, d_send.at[a, k, level], d_recv.at[a, k, level], along_y(k))
             pass_on(a, 1, n, m, view)
@@ -223,6 +232,8 @@
         for m in range(1, parts):
             view = piece(a, n, 0, parts - m)
             arrived(view, y_send.at[a, m, level], y_recv.at[a, m, level])
+            if lines > 1 and (a, n) in LATE_X:
+                send(view, d_send.at[a, m, level], d_recv.at[a, m, level], across)
             pass_on(a, 0, n, m, view)
 
     def from_xy(a, n):
@@ -266,9 +277,8 @@
     own_low()
     for a in range(2):
         own_z(a)
-        own_x(a, 0)
-    for a in range(2):
-        for m in range(1, parts):
+    for m in range(parts):
+        for a in range(2):
             own_x(a, m)
 
     low_here, mid_here, low_total, mid_total = bounds(sl_ref, sm_ref, slices)
@@ -320,7 +330,6 @@
     for view in strains:
         arrived(*view)
     x_full[:before] = jnp.where(y > 0, sh_prev[...], 0.0)
-    spend(1)
     starts = range(0, columns, WIDE)
 
     def mid_tile(start, own):
@@ -359,66 +368,48 @@
         for i in range(lows.shape[0]):
             lows[i] = window(value, i * (WINDOW // RATIO))
 
-    for a in range(2):
-        for n in others[:2]:
-            from_z(a, n)
-    for n in others[:2]:
-        low_from_z(n)
-    spend(3)
-    for n in others[2:]:
-        from_z(0, n)
-        low_from_z(n)
-        from_z(1, n)
-    spend(1)
-    for n in others[:2]:
-        from_x(0, n)
-    spend(1)
-    for n in range(rings):
-        low_from_x(n)
-    from_x(0, 0)
-    spend(1)
-    for n in others[2:]:
-        from_x(0, n)
-    for m in range(1, parts):
-        from_x(0, 0, m)
-    spend(1)
-    low_landed()
-    low_part()
-    for n in others[:2]:
-        from_x(1, n)
-    landed(0, True)
-    mid_filters(True)
-    for n in others[:2]:
-        from_y(0, n)
-    steps = [functools.partial(from_x, 1, n) for n in others[2:]]
-    steps += [functools.partial(from_y, 0, n) for n in others[2:]]
-    steps += [functools.partial(from_xy, 0, n) for n in others]
-    steps += [functools.partial(from_x, 1, 0)]
-    for start in starts:
-        mid_tile(start, True)
-        if steps:
-            steps.pop(0)()
-        spend(1)
-    for step in steps:
-        step()
-        spend(1)
-    for n in others:
-        from_y(1, n)
-    spend(3)
-    for m in range(1, parts):
-        from_x(1, 0, m)
-    landed(1, True)
-    high_filters(True)
-    spend(2)
-    landed(0, False)
-    mid_filters(False)
-    later = list(others)
-    for start in starts:
-        mid_tile(start, False)
-        if later:
-            from_xy(1, later.pop(0))
-    for n in later:
-        from_xy(1, n)
+    left = {own: list(starts) for own in (0, 1)}
+
+    def tiles(own, count):
+        for _ in range(count):
+            if left[own]:
+                mid_tile(left[own].pop(0), own)
+
+    for kind, *at in ORDER:
+        if kind == "f":
+            spend(*at)
+        elif kind == "l":
+            low_landed()
+            low_part()
+        elif kind == "m":
+            if not at[0]:
+                tiles(1, len(starts))
+            landed(0, *at)
+            mid_filters(*at)
+        elif kind == "h":
+            landed(1, *at)
+            high_filters(*at)
+        elif kind == "t":
+            tiles(*at, 1)
+        else:
+            a, first = at
+            for n in range(first, rings if first == 3 else min(first + 1, rings)):
+                if kind == "z":
+                    from_z(a, n)
+                elif kind == "x":
+                    from_x(a, n)
+                elif kind == "y":
+                    from_y(a, n)
+                elif kind == "d":
+                    from_xy(a, n)
+                else:
+                    for m in range(1, parts):
+                        from_x(a, 0, m)
+                if a == 1 and kind == "z":
+                    low_from_z(n)
+                if a == 0 and kind == "x":
+                    low_from_x(n)
+    tiles(0, len(starts))
     spend(len(work))
     landed(1, False)
     high_filters(False)
@@ -619,8 +610,9 @@
                     k = ends_at[n]
                     lead = k * WIDE % WINDOW
                     passes += [(g_ref.at[:, lead : lead + WIDE], (spread.at[(q * across + k) * WIDE // WINDOW],))]
-                for step, (right, lefts) in enumerate(passes):
-                    staged = (n + step) % 2
+                for right, lefts in passes:
+                    staged = turns[q] % 2
+                    turns[q] += 1
                     pltpu.matmul_push_rhs(right[...], staged, q)
                     for turn, left in enumerate(lefts):
                         for r in range(strips):
@@ -628,6 +620,7 @@
                             pltpu.matmul_acc_lhs(acc[r], left[part(r), :], first)
 
         ends_at = {4: 0, 5: 1, 7: 2, 8: 3}
+        turns = [0, 0]
 
         def finish(i, n):
             half = i % 2

time: 42.2 us -> 40.2 us (0.953); the launches traced: 42.1 us -> 39.4 us
  Pallas kernels: 42.1 us -> 39.4 us
    pallas_call x1, Pallas kernels: 31.1 us -> 28.4 us  [gather(): pl.pallas_call(functools.partial(gather_kernel, (bands, peers, slices, li...]
where the time goes in v3:
time: 40.2 us; the launch traced here: 39.4 us
  Pallas kernels  39.4 us (98%)
    pallas_call x1, Pallas kernels, gather(): pl.pallas_call(functools.partial(gather_kernel, (bands, peers, slices, li...  28.4 us
    pallas_call x1, Pallas kernels, compute(): pl.pallas_call(functools.partial(compute_kernel, max(1, tmpl // 64)), out...  11 us

profile of v3, /device:TPU:0, one launch (start us, length us, event | category | flops | bytes accessed | tf_op | source)
XLA Modules:
  0.0 39.4 jit_solution(15942011406670950638)
XLA Ops:
  0.0 28.4 %gather_filters.1 = (bf16[2,9,256,256]{3,2,1,0:T(8,128)(2,1)S(1)}, f32[256,1152]{1,0:T(8,128)S(1)}, bf16[256,512]{1,0:T(8,128)(2,1)S(1)}, bf16[8,9,2,256,256]{4,3,2,1,0:T(8,128)(2,1)S(1)}) custom-call(s32[3]{0:T(128)} %count_ref.1, f32[40,128]{1,0:T(8,128)} %low_ref.1, f32[40,1024]{1,0:T(8,128)} %mid_ref.1, f32[40,1024]{1,0:T(8,128)} %high_ref.1, ...), custom_call_target="tpu_custom_call" | custom-call | tf_op jit(solution)/shard_map/gather_filters/pallas_call | solution.py:511
  28.4 11.0 %filter_templates.1 = f32[1,256,8192]{2,1,0:T(8,128)} custom-call(bf16[2,9,256,256]{3,2,1,0:T(8,128)(2,1)S(1)} %get-tuple-element.9.w_ref, f32[256,1152]{1,0:T(8,128)S(1)} %get-tuple-element.10.p_ref, bf16[256,512]{1,0:T(8,128)(2,1)S(1)} %get-tuple-element.11.g_ref, bf16[8,9,2,256,256]{4,3,2,1,0:T(8,128)(2,1)S(1)} %get-tuple-element.12.frames_ref), custom_call_target="tpu_custom_call" | custom-call | tf_op jit(solution)/shard_map/filter_templates/pallas_call | solution.py:684

commit v4 on v3

--- a/solution.py
+++ b/solution.py
@@ -17,14 +17,14 @@
 SPAN = WINDOW // RATIO + 2 * HALF_TAPS
 MESH = pl.DeviceIdType.MESH
 ORDER = (
-    ("f", 2), ("z", 0, 1), ("z", 0, 2), ("f", 2), ("x", 0, 0), ("f", 1), ("z", 1, 1), ("z", 1, 2), ("f", 5),
-    ("b", 1, 0), ("z", 0, 3), ("f", 1), ("y", 0, 1), ("f", 1), ("x", 0, 1), ("f", 1), ("z", 1, 3), ("f", 1),
-    ("y", 0, 2), ("y", 1, 1), ("x", 0, 2), ("x", 1, 0), ("f", 1), ("b", 0, 0), ("x", 1, 1), ("f", 1), ("y", 1, 2),
-    ("f", 1), ("x", 0, 3), ("l",), ("y", 0, 3), ("f", 2), ("x", 1, 3), ("d", 0, 1), ("m", 1), ("x", 1, 2), ("t", 1),
-    ("t", 1), ("d", 0, 2), ("f", 2), ("y", 1, 3), ("d", 0, 3), ("f", 1), ("t", 1), ("t", 1), ("d", 1, 1), ("t", 1),
-    ("d", 1, 3), ("m", 0), ("t", 0), ("t", 0), ("d", 1, 2), ("t", 0), ("t", 0), ("h", 1), ("t", 0), ("f", 1),
+    ("f", 3), ("x", 0, 0), ("z", 0, 1), ("z", 0, 2), ("f", 2), ("x", 1, 0), ("z", 1, 1), ("z", 1, 2), ("f", 5),
+    ("z", 0, 3), ("y", 0, 1), ("f", 3), ("z", 1, 3), ("f", 1), ("x", 0, 2), ("b", 1, 0), ("x", 0, 1), ("f", 1),
+    ("y", 1, 1), ("f", 2), ("y", 1, 2), ("f", 2), ("x", 0, 3), ("f", 1), ("d", 0, 1), ("x", 1, 2), ("f", 1), ("l",),
+    ("m", 1), ("y", 0, 2), ("y", 0, 3), ("x", 1, 1), ("x", 1, 3), ("t", 1), ("t", 1), ("t", 1), ("d", 0, 2),
+    ("y", 1, 3), ("b", 0, 0), ("d", 0, 3), ("t", 1), ("t", 1), ("d", 1, 1), ("h", 1), ("m", 0), ("t", 0), ("d", 1, 2),
+    ("d", 1, 3), ("t", 0), ("f", 1), ("t", 0), ("t", 0), ("t", 0), ("f", 1),
 )
-LATE_X = ((0, 2), (1, 1))
+LATE_X = ((0, 1), (1, 1))
 
 
 def upsample_matrix():

time: 40.2 us -> 39.4 us (0.980); the launches traced: 39.4 us -> 39.3 us
  no operation moved by 1% of the time
where the time goes in v4:
time: 39.4 us; the launch traced here: 39.3 us
  Pallas kernels  39.3 us (100%)
    pallas_call x1, Pallas kernels, gather(): pl.pallas_call(functools.partial(gather_kernel, (bands, peers, slices, li...  28.3 us
    pallas_call x1, Pallas kernels, compute(): pl.pallas_call(functools.partial(compute_kernel, max(1, tmpl // 64)), out...  11 us

profile of v4, /device:TPU:0, one launch (start us, length us, event | category | flops | bytes accessed | tf_op | source)
XLA Modules:
  0.0 39.3 jit_solution(10719430450205917507)
XLA Ops:
  0.0 28.3 %gather_filters.1 = (bf16[2,9,256,256]{3,2,1,0:T(8,128)(2,1)S(1)}, f32[256,1152]{1,0:T(8,128)S(1)}, bf16[256,512]{1,0:T(8,128)(2,1)S(1)}, bf16[8,9,2,256,256]{4,3,2,1,0:T(8,128)(2,1)S(1)}) custom-call(s32[3]{0:T(128)} %count_ref.1, f32[40,128]{1,0:T(8,128)} %low_ref.1, f32[40,1024]{1,0:T(8,128)} %mid_ref.1, f32[40,1024]{1,0:T(8,128)} %high_ref.1, ...), custom_call_target="tpu_custom_call" | custom-call | tf_op jit(solution)/shard_map/gather_filters/pallas_call | solution.py:511
  28.3 11.0 %filter_templates.1 = f32[1,256,8192]{2,1,0:T(8,128)} custom-call(bf16[2,9,256,256]{3,2,1,0:T(8,128)(2,1)S(1)} %get-tuple-element.9.w_ref, f32[256,1152]{1,0:T(8,128)S(1)} %get-tuple-element.10.p_ref, bf16[256,512]{1,0:T(8,128)(2,1)S(1)} %get-tuple-element.11.g_ref, bf16[8,9,2,256,256]{4,3,2,1,0:T(8,128)(2,1)S(1)} %get-tuple-element.12.frames_ref), custom_call_target="tpu_custom_call" | custom-call | tf_op jit(solution)/shard_map/filter_templates/pallas_call | solution.py:684
